TPU v7x, 32 devices: a whole 2x2x4 slice. The times are simulated.
32 devices in a mesh: member: 2 (over x), tile: 16 (over z, y, core).
Axes of the slice: x: 2, y: 2, z: 4, core: 2. Of those that a mesh axis runs over, the one named last changes fastest.
Arguments:
- pressure: float32 [64, 128, 512], P('member', 'tile'), parts along dimension 0, may hold values from -1.5 to 1
- conductivity: float32 [64, 128, 512], P('member', 'tile'), parts along dimension 0, may hold values from 0.5 to 2
- soil_class: int32 [64, 128, 512], P('member', 'tile'), parts along dimension 0, may hold values from 0 to 11
- vg_alpha: float32 [12], replicated, may hold values from 0.3 to 2
- vg_shape: float32 [12], replicated, may hold values from 1.3 to 2.6
- bed: float32 [512, 256], P('tile', 'member'), parts along dimension 1, may hold values from -4 to 4
- flow_code: int32 [512, 256], P('tile', 'member'), parts along dimension 1, may hold values from 0 to 7
- surface_soil: int32 [512, 256], P('tile', 'member'), parts along dimension 1, may hold values from 0 to 11
- cover_class: int32 [512, 256], P('tile', 'member'), parts along dimension 1, may hold values from 0 to 16
- ponding: int32 [512, 256], P('tile', 'member'), parts along dimension 1, may hold values 0 or 1
- conveyance: float32 [17], replicated, may hold values from 0.3 to 3
- erodibility: float32 [12], replicated, may hold values from 0.1 to 1
Outputs:
- head_out: float32 [64, 128, 512], P('member', 'tile'), parts along dimension 0
- bed_out: float32 [512, 256], P('tile', 'member'), parts along dimension 1
There are 2 independent parts, one for each index of `member`. A program takes and returns all parts, laid end to end along the dimension named above; an argument that names none is the same for every part. Nothing has to cross between parts.
All inputs are finite; a program needn't handle non-finite values. No bound on the sum of `ponding` on one device may be relied on, other than what follows from the above.
Results may differ from a plain program's by a relative error of at most 0.00035.
Values sent between devices are 32-bit elements; how exact they have to be, the bound alone decides.
A program may use at most 128 MiB of HBM per device.

v0:
```python
import functools
import math

import jax
import jax.numpy as jnp
from jax import lax
from jax.experimental import pallas as pl
from jax.experimental.pallas import tpu as pltpu
from jax.sharding import PartitionSpec as P

STEPS = 4
RELAX_STEP = 0.08
CAPACITY = 2.0
MIN_SLOPE = 0.01
BED_RATE = 2.0
SHIFT_X = (1, 1, 0, -1, -1, -1, 0, 1)
SHIFT_Y = (0, 1, 1, 1, 0, -1, -1, -1)
TINY = 1.2e-38
LANES = 128
HEAD_A, HEAD_B, DEPTH, LEVEL, SOIL_K, SOIL_C = range(6)


def table_pick(classes, table, entries):
    picked = jnp.full(classes.shape, table(0), jnp.float32)
    for entry in range(1, entries):
        picked = jnp.where(classes == entry, table(entry), picked)
    return picked


def turn(values, shift, axis):
    shift = shift % values.shape[axis]
    return values if shift == 0 else pltpu.roll(values, shift, axis)


def kernel(
    count,
    head_in,
    ks_in,
    class_in,
    alpha_t,
    shape_t,
    bed_in,
    code_in,
    soil_in,
    cover_in,
    pond_in,
    convey_t,
    erod_t,
    head_out,
    bed_out,
    head_a,
    head_b,
    half_k,
    gain,
    ks,
    alpha,
    shape,
    half_m,
    levels,
    depths,
    maps,
    classes,
    packed,
    gathered,
    final_src,
    final_dst,
    turned,
    send_sem,
    recv_sem,
    spread_send,
    spread_recv,
    final_send,
    final_recv,
):
    rows, layers, columns = head_in.shape
    strip = bed_in.shape[0]
    width = bed_in.shape[1]
    per = LANES // strip
    groups = columns // LANES
    me = lax.axis_index("tile")
    has_left = me > 0
    has_right = me < count - 1
    low = 1 - (me + count - 1) // count
    high = rows + (2 * count - 2 - me) // count

    def at(tile):
        return {"tile": tile}

    def to_left(kind, src, dst):
        return pltpu.make_async_remote_copy(
            src_ref=src,
            dst_ref=dst,
            send_sem=send_sem.at[kind, 0],
            recv_sem=recv_sem.at[kind, 1],
            device_id=at(me - 1),
            device_id_type=pl.DeviceIdType.MESH,
        )

    def to_right(kind, src, dst):
        return pltpu.make_async_remote_copy(
            src_ref=src,
            dst_ref=dst,
            send_sem=send_sem.at[kind, 1],
            recv_sem=recv_sem.at[kind, 0],
            device_id=at(me + 1),
            device_id_type=pl.DeviceIdType.MESH,
        )

    def push(kind, first, last, low_halo, high_halo):
        @pl.when(has_left)
        def _():
            to_left(kind, first, high_halo).start()

        @pl.when(has_right)
        def _():
            to_right(kind, last, low_halo).start()

    def await_recv(kind, low_halo, high_halo):
        @pl.when(has_left)
        def _():
            to_right(kind, low_halo, low_halo).wait_recv()

        @pl.when(has_right)
        def _():
            to_left(kind, high_halo, high_halo).wait_recv()

    def await_send(kind, first, last):
        @pl.when(has_left)
        def _():
            to_left(kind, first, first).wait_send()

        @pl.when(has_right)
        def _():
            to_right(kind, last, last).wait_send()

    levels[...] = jnp.zeros_like(levels)
    depths[...] = jnp.zeros_like(depths)

    coef_y = table_pick(cover_in[...], lambda i: convey_t[i], convey_t.shape[0]) * (
        1.0 - pond_in[...].astype(jnp.float32)
    )
    erode_y = table_pick(soil_in[...], lambda i: erod_t[i], erod_t.shape[0])
    stacked = jnp.concatenate(
        [coef_y, erode_y, code_in[...].astype(jnp.float32), bed_in[...]], axis=0
    )
    packed[0:rows] = jnp.zeros((rows, LANES), jnp.float32)
    packed[rows + width : 2 * rows + width] = jnp.zeros((rows, LANES), jnp.float32)
    for block in range(width // LANES):
        packed[rows + block * LANES : rows + (block + 1) * LANES] = jnp.transpose(
            stacked[:, block * LANES : (block + 1) * LANES]
        )

    barrier = pltpu.get_barrier_semaphore()
    for away in range(1, count):
        pl.semaphore_signal(
            barrier,
            inc=1,
            device_id=at(lax.rem(me + away, count)),
            device_id_type=pl.DeviceIdType.MESH,
        )
    pl.semaphore_wait(barrier, count - 1)

    last_row = rows + 1
    push(SOIL_C, class_in.at[0], class_in.at[rows - 1], classes.at[0], classes.at[1])
    push(SOIL_K, ks_in.at[0], ks_in.at[rows - 1], ks.at[0], ks.at[last_row])
    push(HEAD_A, head_in.at[0], head_in.at[rows - 1], head_a.at[0], head_a.at[last_row])

    def spread(away):
        peer = lax.rem(me + away, count)
        return pltpu.make_async_remote_copy(
            src_ref=packed.at[pl.ds(pl.multiple_of(peer * rows, rows), 3 * rows)],
            dst_ref=gathered.at[me],
            send_sem=spread_send.at[away],
            recv_sem=spread_recv.at[away],
            device_id=at(peer),
            device_id_type=pl.DeviceIdType.MESH,
        )

    for away in range(1, count):
        spread(away).start()
    gathered[me] = packed[pl.ds(pl.multiple_of(me * rows, rows), 3 * rows)]

    def soil_row(row, found):
        alpha[row] = table_pick(found, lambda i: alpha_t[i], alpha_t.shape[0])
        bend = table_pick(found, lambda i: shape_t[i], shape_t.shape[0])
        shape[row] = bend
        half_m[row] = 0.5 / bend - 0.5

    @pl.loop(0, rows)
    def _(row):
        soil_row(row + 1, class_in[row])
        ks[row + 1] = 0.5 * ks_in[row]
        head_a[row + 1] = head_in[row]

    def conduct_row(head, row, keep):
        bend = shape[row]
        log_a = lax.log2(alpha[row] * jnp.maximum(-head[row], TINY))
        log_w = lax.log2(1.0 + lax.exp2(bend * log_a))
        root = lax.exp2(half_m[row] * log_w)
        full = root * root
        inner = 1.0 - lax.exp2((bend - 1.0) * log_a) * full
        half_k[row] = ks[row] * root * (inner * inner)
        if keep:
            gain[row] = RELAX_STEP / (1.0 + CAPACITY * (1.0 - full))

    layer = lax.broadcasted_iota(jnp.int32, (layers, columns), 0)
    lane = lax.broadcasted_iota(jnp.int32, (layers, columns), 1)

    def flow_row(src, dst, row, below, above):
        k = half_k[row]
        h = src[row]
        flow = (k + half_k[above]) * (src[above] - h) + (k + half_k[below]) * (src[below] - h)
        side = (k + turn(k, -1, 1)) * (turn(h, -1, 1) - h)
        side = jnp.where(lane == columns - 1, 0.0, side)
        flow = flow + side - turn(side, 1, 1)
        down = (k + turn(k, -1, 0)) * (turn(h, -1, 0) - h - 1.0)
        down = jnp.where(layer == layers - 1, 0.0, down)
        flow = flow + down - turn(down, 1, 0)
        flow = flow - jnp.where(layer == layers - 1, 2.0 * k, 0.0)
        dst[row] = h + flow * gain[row]

    def sweep(src, dst, before_edges, after_edges):
        @pl.loop(1, rows + 1)
        def _(row):
            conduct_row(src, row, True)

        before_edges()
        conduct_row(src, 0, False)
        conduct_row(src, last_row, False)
        flow_row(src, dst, 1, low, 2)
        flow_row(src, dst, rows, rows - 1, high)
        after_edges()

        @pl.loop(2, rows)
        def _(row):
            flow_row(src, dst, row, row - 1, row + 1)

    await_recv(SOIL_C, classes.at[0], classes.at[1])
    await_recv(SOIL_K, ks.at[0], ks.at[last_row])
    soil_row(0, classes[0])
    soil_row(last_row, classes[1])
    ks[0] = 0.5 * ks[0]
    ks[last_row] = 0.5 * ks[last_row]
    await_recv(HEAD_A, head_a.at[0], head_a.at[last_row])
    await_send(SOIL_C, class_in.at[0], class_in.at[rows - 1])
    await_send(SOIL_K, ks_in.at[0], ks_in.at[rows - 1])
    await_send(HEAD_A, head_in.at[0], head_in.at[rows - 1])

    own = slice(rows, 2 * rows)
    wide_lane = lax.broadcasted_iota(jnp.int32, (3 * rows, columns), 1)
    piece = lax.broadcasted_iota(jnp.int32, (3 * rows, LANES), 1) // strip

    def assemble():
        for away in range(1, count):
            spread(away).wait()
        for group in range(groups):
            for kind in range(4):
                joined = None
                for part in range(per):
                    block = turn(gathered[group * per + part], (part - kind) * strip, 1)
                    joined = block if joined is None else jnp.where(piece == part, block, joined)
                spot = slice(group * LANES, (group + 1) * LANES)
                if kind < 3:
                    maps[kind, :, spot] = joined
                else:
                    levels[0, :, spot] = joined

    def shifted(values, first, second):
        values = turn(values, -second, 1)
        if second == 1:
            values = jnp.where(wide_lane == columns - 1, 0.0, values)
        if second == -1:
            values = jnp.where(wide_lane == 0, 0.0, values)
        return turn(values, -first, 0)

    def surface(level, depth):
        coef, erode, code = maps[0], maps[1], maps[2]
        target = jnp.zeros_like(level)
        scale = jnp.ones_like(level)
        for course in range(8):
            first, second = SHIFT_X[course], SHIFT_Y[course]
            chosen = code == course
            target = jnp.where(chosen, shifted(level, first, second), target)
            if first * second != 0:
                scale = jnp.where(chosen, 1.0 / math.sqrt(2.0), scale)
        slope = MIN_SLOPE + jnp.maximum(level - target, 0.0) * scale
        root = jnp.sqrt(slope)
        power = lax.exp2((2.0 / 3.0) * lax.log2(jnp.maximum(depth, TINY)))
        drive = coef * root * power
        outflow = depth * drive / (1.0 + drive)
        sediment = erode * outflow * root
        sums = []
        for field in (outflow, sediment):
            total = -field
            for course in range(8):
                sent = jnp.where(code == course, field, 0.0)
                total = total + shifted(sent, -SHIFT_X[course], -SHIFT_Y[course])
            sums.append(total)
        return sums[0], BED_RATE * sums[1]

    @pl.loop(0, STEPS)
    def _(step):
        slot = lax.rem(step, 2)
        other = 1 - slot
        going = step < STEPS - 1

        def push_b():
            push(HEAD_B, head_b.at[1], head_b.at[rows], head_b.at[0], head_b.at[last_row])

        def take_b():
            await_recv(HEAD_B, head_b.at[0], head_b.at[last_row])
            await_send(HEAD_B, head_b.at[1], head_b.at[rows])

        def push_a():
            @pl.when(going)
            def _():
                push(HEAD_A, head_a.at[1], head_a.at[rows], head_a.at[0], head_a.at[last_row])

        sweep(head_a, head_b, lambda: None, push_b)
        sweep(head_b, head_a, take_b, push_a)

        @pl.when(step == 0)
        def _():
            assemble()

        low_level = levels.at[slot, 0:rows]
        own_level = levels.at[slot, own]
        high_level = levels.at[slot, 2 * rows : 3 * rows]

        @pl.when(step > 0)
        def _():
            await_recv(LEVEL, low_level, high_level)
            await_send(LEVEL, own_level, own_level)

        for row in range(rows):
            depths[rows + row : rows + row + 1] = jnp.maximum(head_a[row + 1, 0:1, :], 0.0)
        low_depth = depths.at[0:rows]
        own_depth = depths.at[own]
        high_depth = depths.at[2 * rows : 3 * rows]
        push(DEPTH, own_depth, own_depth, low_depth, high_depth)
        await_recv(DEPTH, low_depth, high_depth)
        await_send(DEPTH, own_depth, own_depth)

        @pl.when(going)
        def _():
            await_recv(HEAD_A, head_a.at[0], head_a.at[last_row])
            await_send(HEAD_A, head_a.at[1], head_a.at[rows])

        change, bed_change = surface(levels[slot], depths[...])
        for row in range(rows + 2):
            top = head_a[row, 0:1, :]
            head_a[row, 0:1, :] = top + change[rows - 1 + row : rows + row]
        levels[other, own] = levels[slot, own] + bed_change[own]

        @pl.when(going)
        def _():
            next_level = levels.at[other, own]
            push(
                LEVEL,
                next_level,
                next_level,
                levels.at[other, 0:rows],
                levels.at[other, 2 * rows : 3 * rows],
            )

    for group in range(groups):
        final_src[group] = levels[STEPS % 2, own, group * LANES : (group + 1) * LANES]

    def finish(away):
        peer = lax.rem(me + away, count)
        return pltpu.make_async_remote_copy(
            src_ref=final_src.at[peer // per],
            dst_ref=final_dst.at[me],
            send_sem=final_send.at[away],
            recv_sem=final_recv.at[away],
            device_id=at(peer),
            device_id_type=pl.DeviceIdType.MESH,
        )

    for away in range(1, count):
        finish(away).start()
    final_dst[me] = final_src[me // per]
    head_out[...] = head_a[1 : rows + 1]
    for away in range(1, count):
        finish(away).wait()
    members = LANES // rows
    for block in range(width // LANES):
        part = final_dst[block * members : (block + 1) * members]
        turned[:, block * LANES : (block + 1) * LANES] = jnp.transpose(
            part.reshape(LANES, LANES)
        )
    start = pl.multiple_of(lax.rem(me, per) * strip, strip)
    bed_out[...] = turned[pl.ds(start, strip)]


def on_device(
    pressure,
    conductivity,
    soil_class,
    vg_alpha,
    vg_shape,
    bed,
    flow_code,
    surface_soil,
    cover_class,
    ponding,
    conveyance,
    erodibility,
):
    count = lax.axis_size("tile")
    layers, rows, columns = pressure.shape
    strip, width = bed.shape
    head = jnp.swapaxes(pressure, 0, 1)
    ks = jnp.swapaxes(conductivity, 0, 1)
    classes = jnp.swapaxes(soil_class, 0, 1).astype(jnp.float32)
    vmem = pl.BlockSpec(memory_space=pltpu.VMEM)
    smem = pl.BlockSpec(memory_space=pltpu.SMEM)
    wide = pltpu.VMEM((rows + 2, layers, columns), jnp.float32)
    dma = pltpu.SemaphoreType.DMA
    head_out, bed_out = pl.pallas_call(
        functools.partial(kernel, count),
        out_shape=(
            jax.ShapeDtypeStruct((rows, layers, columns), jnp.float32),
            jax.ShapeDtypeStruct((strip, width), jnp.float32),
        ),
        in_specs=[vmem, vmem, vmem, smem, smem, vmem, vmem, vmem, vmem, vmem, smem, smem],
        out_specs=(vmem, vmem),
        scratch_shapes=[
            wide,
            wide,
            wide,
            wide,
            wide,
            wide,
            wide,
            wide,
            pltpu.VMEM((2, 3 * rows, columns), jnp.float32),
            pltpu.VMEM((3 * rows, columns), jnp.float32),
            pltpu.VMEM((3, 3 * rows, columns), jnp.float32),
            pltpu.VMEM((2, layers, columns), jnp.float32),
            pltpu.VMEM((width + 2 * rows, LANES), jnp.float32),
            pltpu.VMEM((count, 3 * rows, LANES), jnp.float32),
            pltpu.VMEM((columns // LANES, rows, LANES), jnp.float32),
            pltpu.VMEM((count, rows, LANES), jnp.float32),
            pltpu.VMEM((LANES, width), jnp.float32),
            dma((6, 2)),
            dma((6, 2)),
            dma((count,)),
            dma((count,)),
            dma((count,)),
            dma((count,)),
        ],
        compiler_params=pltpu.CompilerParams(
            collective_id=0, has_side_effects=True, vmem_limit_bytes=40 * 1024 * 1024
        ),
    )(
        head,
        ks,
        classes,
        vg_alpha,
        vg_shape,
        bed,
        flow_code,
        surface_soil,
        cover_class,
        ponding,
        conveyance,
        erodibility,
    )
    return jnp.swapaxes(head_out, 0, 1), bed_out


def solution(mesh):
    in_specs = (
        P("member", "tile", None),
        P("member", "tile", None),
        P("member", "tile", None),
        P(),
        P(),
        P("tile", "member"),
        P("tile", "member"),
        P("tile", "member"),
        P("tile", "member"),
        P("tile", "member"),
        P(),
        P(),
    )
    out_specs = (P("member", "tile", None), P("tile", "member"))
    return jax.shard_map(
        on_device, mesh=mesh, in_specs=in_specs, out_specs=out_specs, check_vma=False
    )
```

profile of v0, /device:TPU:0, one launch (start us, length us, event | category | flops | bytes accessed | tf_op | source)
XLA Modules:
  0.0 57.6 jit_solution(15366597037385728735)
XLA Ops:
  0.6 0.0 copy-start.9
  0.6 0.0 copy-start.10
  0.6 1.4 %fusion.class_in = f32[8,32,512]{2,1,0:T(8,128)S(1)} fusion(s32[32,8,512]{2,1,0:T(8,128)} %param.14), kind=kLoop, calls=%fused_computation.1 | loop fusion | flops 131072 | bytes 1048576 | tf_op jit(solution)/shard_map/convert_element_type | solution.py:415
  2.1 0.0 copy-start
  2.1 0.0 copy-start.1
  2.1 0.0 copy-start.2
  2.1 0.0 copy-start.3
  2.2 0.0 copy-start.4
  2.2 0.0 copy-start.8
  2.2 0.6 %copy_bitcast_fusion = (f32[8,32,512]{2,1,0:T(8,128)S(1)}, f32[8,32,512]{2,1,0:T(8,128)S(1)}) fusion(f32[32,8,512]{2,1,0:T(8,128)S(1)} %copy-done.9, f32[32,8,512]{2,1,0:T(8,128)S(1)} %copy-done.10), kind=kLoop, calls=%fused_computation.2 | loop fusion | bytes 2097152 | tf_op jit(solution)/shard_map/transpose | solution.py:414
  2.8 0.0 copy-start.5
  2.8 0.0 copy-start.6
  2.8 0.0 copy-start.7
  2.8 0.0 copy-done
  2.8 0.0 copy-done.1
  2.9 0.0 copy-done.2
  2.9 0.0 copy-done.3
  2.9 0.0 copy-done.4
  2.9 0.6 copy-done.5
  3.5 0.0 copy-done.6
  3.5 0.0 copy-done.7
  3.5 52.4 %shard_map.131 = (f32[8,32,512]{2,1,0:T(8,128)S(1)}, f32[32,128]{1,0:T(8,128)S(1)}) custom-call(f32[8,32,512]{2,1,0:T(8,128)S(1)} %get-tuple-element.9.head_in, f32[8,32,512]{2,1,0:T(8,128)S(1)} %get-tuple-element.8.ks_in, f32[8,32,512]{2,1,0:T(8,128)S(1)} %fusion.class_in, f32[12]{0:T(128)S(1)} %copy-done.5, f32[12]{0:T(128)S(1)} %copy-done.6, ...), custom_call_target="tpu_custom_call" | custom-call | tf_op jit(solution)/shard_map/pallas_call | solution.py:420
  55.9 1.1 %copy.17 = f32[32,8,512]{2,1,0:T(8,128)} copy(f32[32,8,512]{2,0,1:T(8,128)S(1)} %bitcast.7) | data formatting | bytes 1048576
  57.0 0.6 %copy.24 = f32[32,128]{1,0:T(8,128)} copy(f32[32,128]{1,0:T(8,128)S(1)} %get-tuple-element.13) | data formatting | bytes 32768
  (3 shorter events, 0.0 us)
Async XLA Ops:
  0.6 1.5 %copy-start.9 = (f32[32,8,512]{2,1,0:T(8,128)S(1)}, f32[32,8,512]{2,1,0:T(8,128)}, u32[]{:S(2)}) copy-start(f32[32,8,512]{2,1,0:T(8,128)} %param.13) | copy-start | bytes 1572868
  0.6 1.5 %copy-start.10 = (f32[32,8,512]{2,1,0:T(8,128)S(1)}, f32[32,8,512]{2,1,0:T(8,128)}, u32[]{:S(2)}) copy-start(f32[32,8,512]{2,1,0:T(8,128)} %param.12) | copy-start | bytes 1572868
  2.1 0.7 %copy-start = (f32[32,128]{1,0:T(8,128)S(1)}, f32[32,128]{1,0:T(8,128)}, u32[]{:S(2)}) copy-start(f32[32,128]{1,0:T(8,128)} %bed_in.1) | copy-start | bytes 49156
  2.1 0.7 %copy-start.1 = (s32[32,128]{1,0:T(8,128)S(1)}, s32[32,128]{1,0:T(8,128)}, u32[]{:S(2)}) copy-start(s32[32,128]{1,0:T(8,128)} %code_in.1) | copy-start | bytes 49156
  2.1 0.7 %copy-start.2 = (s32[32,128]{1,0:T(8,128)S(1)}, s32[32,128]{1,0:T(8,128)}, u32[]{:S(2)}) copy-start(s32[32,128]{1,0:T(8,128)} %soil_in.1) | copy-start | bytes 49156
  2.1 0.7 %copy-start.3 = (s32[32,128]{1,0:T(8,128)S(1)}, s32[32,128]{1,0:T(8,128)}, u32[]{:S(2)}) copy-start(s32[32,128]{1,0:T(8,128)} %cover_in.1) | copy-start | bytes 49156
  2.2 0.7 %copy-start.4 = (s32[32,128]{1,0:T(8,128)S(1)}, s32[32,128]{1,0:T(8,128)}, u32[]{:S(2)}) copy-start(s32[32,128]{1,0:T(8,128)} %pond_in.1) | copy-start | bytes 49156
  2.2 0.7 %copy-start.8 = (f32[12]{0:T(128)S(1)}, f32[12]{0:T(128)}, u32[]{:S(2)}) copy-start(f32[12]{0:T(128)} %erod_t.1) | copy-start | bytes 148
  2.8 0.7 %copy-start.5 = (f32[12]{0:T(128)S(1)}, f32[12]{0:T(128)}, u32[]{:S(2)}) copy-start(f32[12]{0:T(128)} %alpha_t.1) | copy-start | bytes 148
  2.8 0.7 %copy-start.6 = (f32[12]{0:T(128)S(1)}, f32[12]{0:T(128)}, u32[]{:S(2)}) copy-start(f32[12]{0:T(128)} %shape_t.1) | copy-start | bytes 148
  2.8 0.7 %copy-start.7 = (f32[17]{0:T(128)S(1)}, f32[17]{0:T(128)}, u32[]{:S(2)}) copy-start(f32[17]{0:T(128)} %convey_t.1) | copy-start | bytes 208
where the time goes:
time: 57.8 us; the launch traced here: 57.6 us
  Pallas kernels  52.4 us (91%)
  local copies, waits for them, and re-layouts  3 us (5%)
  other arithmetic  1.44 us (2%)
  between operations  0.77 us (1%)
    pallas_call x1, Pallas kernels, on_device(): pl.pallas_call(functools.partial(kernel, count), out_shape=(jax.ShapeDtyp...  52.4 us
    unnamed x24, local copies, waits for them, and re-layouts  2.39 us
    convert_element_type x1, other arithmetic, on_device(): classes = jnp.swapaxes(soil_class, 0, 1).astype(jnp.float32)  1.44 us

commit v1 on v0

--- a/solution.py
+++ b/solution.py
@@ -17,7 +17,9 @@
 SHIFT_Y = (0, 1, 1, 1, 0, -1, -1, -1)
 TINY = 1.2e-38
 LANES = 128
-HEAD_A, HEAD_B, DEPTH, LEVEL, SOIL_K, SOIL_C = range(6)
+TOPS, REST, LEVEL, SOIL_K, SOIL_C = range(5)
+HALO = 2
+TOP = 8
 
 
 def table_pick(classes, table, entries):
@@ -60,6 +62,8 @@
     depths,
     maps,
     classes,
+    tops,
+    rest,
     packed,
     gathered,
     final_src,
@@ -80,75 +84,58 @@
     me = lax.axis_index("tile")
     has_left = me > 0
     has_right = me < count - 1
-    low = 1 - (me + count - 1) // count
-    high = rows + (2 * count - 2 - me) // count
+    first = HALO
+    last = rows + HALO - 1
+    total_rows = rows + 2 * HALO
+    low = first - (me + count - 1) // count
+    high = last + (2 * count - 2 - me) // count
 
     def at(tile):
         return {"tile": tile}
 
-    def to_left(kind, src, dst):
+    def to_left(kind, slot, src, dst):
         return pltpu.make_async_remote_copy(
             src_ref=src,
             dst_ref=dst,
-            send_sem=send_sem.at[kind, 0],
-            recv_sem=recv_sem.at[kind, 1],
+            send_sem=send_sem.at[kind, slot, 0],
+            recv_sem=recv_sem.at[kind, slot, 1],
             device_id=at(me - 1),
             device_id_type=pl.DeviceIdType.MESH,
         )
 
-    def to_right(kind, src, dst):
+    def to_right(kind, slot, src, dst):
         return pltpu.make_async_remote_copy(
             src_ref=src,
             dst_ref=dst,
-            send_sem=send_sem.at[kind, 1],
-            recv_sem=recv_sem.at[kind, 0],
+            send_sem=send_sem.at[kind, slot, 1],
+            recv_sem=recv_sem.at[kind, slot, 0],
             device_id=at(me + 1),
             device_id_type=pl.DeviceIdType.MESH,
         )
 
-    def push(kind, first, last, low_halo, high_halo):
+    def push(kind, slot, for_left, for_right, low_halo, high_halo):
         @pl.when(has_left)
         def _():
-            to_left(kind, first, high_halo).start()
+            to_left(kind, slot, for_left, high_halo).start()
 
         @pl.when(has_right)
         def _():
-            to_right(kind, last, low_halo).start()
-
-    def await_recv(kind, low_halo, high_halo):
+            to_right(kind, slot, for_right, low_halo).start()
+
+    def settle(kind, slot, low_halo, high_halo):
         @pl.when(has_left)
         def _():
-            to_right(kind, low_halo, low_halo).wait_recv()
+            to_right(kind, slot, low_halo, low_halo).wait_recv()
+            to_left(kind, slot, low_halo, low_halo).wait_send()
 
         @pl.when(has_right)
         def _():
-            to_left(kind, high_halo, high_halo).wait_recv()
-
-    def await_send(kind, first, last):
-        @pl.when(has_left)
-        def _():
-            to_left(kind, first, first).wait_send()
-
-        @pl.when(has_right)
-        def _():
-            to_right(kind, last, last).wait_send()
+            to_left(kind, slot, high_halo, high_halo).wait_recv()
+            to_right(kind, slot, high_halo, high_halo).wait_send()
 
     levels[...] = jnp.zeros_like(levels)
     depths[...] = jnp.zeros_like(depths)
-
-    coef_y = table_pick(cover_in[...], lambda i: convey_t[i], convey_t.shape[0]) * (
-        1.0 - pond_in[...].astype(jnp.float32)
-    )
-    erode_y = table_pick(soil_in[...], lambda i: erod_t[i], erod_t.shape[0])
-    stacked = jnp.concatenate(
-        [coef_y, erode_y, code_in[...].astype(jnp.float32), bed_in[...]], axis=0
-    )
-    packed[0:rows] = jnp.zeros((rows, LANES), jnp.float32)
-    packed[rows + width : 2 * rows + width] = jnp.zeros((rows, LANES), jnp.float32)
-    for block in range(width // LANES):
-        packed[rows + block * LANES : rows + (block + 1) * LANES] = jnp.transpose(
-            stacked[:, block * LANES : (block + 1) * LANES]
-        )
+    tops[...] = jnp.zeros_like(tops)
 
     barrier = pltpu.get_barrier_semaphore()
     for away in range(1, count):
@@ -158,27 +145,19 @@
             device_id=at(lax.rem(me + away, count)),
             device_id_type=pl.DeviceIdType.MESH,
         )
-    pl.semaphore_wait(barrier, count - 1)
-
-    last_row = rows + 1
-    push(SOIL_C, class_in.at[0], class_in.at[rows - 1], classes.at[0], classes.at[1])
-    push(SOIL_K, ks_in.at[0], ks_in.at[rows - 1], ks.at[0], ks.at[last_row])
-    push(HEAD_A, head_in.at[0], head_in.at[rows - 1], head_a.at[0], head_a.at[last_row])
-
-    def spread(away):
-        peer = lax.rem(me + away, count)
-        return pltpu.make_async_remote_copy(
-            src_ref=packed.at[pl.ds(pl.multiple_of(peer * rows, rows), 3 * rows)],
-            dst_ref=gathered.at[me],
-            send_sem=spread_send.at[away],
-            recv_sem=spread_recv.at[away],
-            device_id=at(peer),
-            device_id_type=pl.DeviceIdType.MESH,
-        )
-
-    for away in range(1, count):
-        spread(away).start()
-    gathered[me] = packed[pl.ds(pl.multiple_of(me * rows, rows), 3 * rows)]
+    coef_y = table_pick(cover_in[...], lambda i: convey_t[i], convey_t.shape[0]) * (
+        1.0 - pond_in[...].astype(jnp.float32)
+    )
+    erode_y = table_pick(soil_in[...], lambda i: erod_t[i], erod_t.shape[0])
+    stacked = jnp.concatenate(
+        [coef_y, erode_y, code_in[...].astype(jnp.float32), bed_in[...]], axis=0
+    )
+    packed[0:rows] = jnp.zeros((rows, LANES), jnp.float32)
+    packed[rows + width : 2 * rows + width] = jnp.zeros((rows, LANES), jnp.float32)
+    for block in range(width // LANES):
+        packed[rows + block * LANES : rows + (block + 1) * LANES] = jnp.transpose(
+            stacked[:, block * LANES : (block + 1) * LANES]
+        )
 
     def soil_row(row, found):
         alpha[row] = table_pick(found, lambda i: alpha_t[i], alpha_t.shape[0])
@@ -186,22 +165,15 @@
         shape[row] = bend
         half_m[row] = 0.5 / bend - 0.5
 
-    @pl.loop(0, rows)
-    def _(row):
-        soil_row(row + 1, class_in[row])
-        ks[row + 1] = 0.5 * ks_in[row]
-        head_a[row + 1] = head_in[row]
-
-    def conduct_row(head, row, keep):
-        bend = shape[row]
-        log_a = lax.log2(alpha[row] * jnp.maximum(-head[row], TINY))
+    def conduct_row(head, row, part):
+        bend = shape[row, part]
+        log_a = lax.log2(alpha[row, part] * jnp.maximum(-head[row, part], TINY))
         log_w = lax.log2(1.0 + lax.exp2(bend * log_a))
-        root = lax.exp2(half_m[row] * log_w)
+        root = lax.exp2(half_m[row, part] * log_w)
         full = root * root
         inner = 1.0 - lax.exp2((bend - 1.0) * log_a) * full
-        half_k[row] = ks[row] * root * (inner * inner)
-        if keep:
-            gain[row] = RELAX_STEP / (1.0 + CAPACITY * (1.0 - full))
+        half_k[row, part] = ks[row, part] * root * (inner * inner)
+        gain[row, part] = RELAX_STEP / (1.0 + CAPACITY * (1.0 - full))
 
     layer = lax.broadcasted_iota(jnp.int32, (layers, columns), 0)
     lane = lax.broadcasted_iota(jnp.int32, (layers, columns), 1)
@@ -219,32 +191,58 @@
         flow = flow - jnp.where(layer == layers - 1, 2.0 * k, 0.0)
         dst[row] = h + flow * gain[row]
 
-    def sweep(src, dst, before_edges, after_edges):
-        @pl.loop(1, rows + 1)
+    whole_part = slice(0, layers)
+    top_part = slice(0, TOP)
+    rest_part = slice(TOP, layers)
+
+    def conduct_rows(head, start, stop, part):
+        @pl.loop(start, stop, unroll=True)
         def _(row):
-            conduct_row(src, row, True)
-
-        before_edges()
-        conduct_row(src, 0, False)
-        conduct_row(src, last_row, False)
-        flow_row(src, dst, 1, low, 2)
-        flow_row(src, dst, rows, rows - 1, high)
-        after_edges()
-
-        @pl.loop(2, rows)
-        def _(row):
-            flow_row(src, dst, row, row - 1, row + 1)
-
-    await_recv(SOIL_C, classes.at[0], classes.at[1])
-    await_recv(SOIL_K, ks.at[0], ks.at[last_row])
-    soil_row(0, classes[0])
-    soil_row(last_row, classes[1])
-    ks[0] = 0.5 * ks[0]
-    ks[last_row] = 0.5 * ks[last_row]
-    await_recv(HEAD_A, head_a.at[0], head_a.at[last_row])
-    await_send(SOIL_C, class_in.at[0], class_in.at[rows - 1])
-    await_send(SOIL_K, ks_in.at[0], ks_in.at[rows - 1])
-    await_send(HEAD_A, head_in.at[0], head_in.at[rows - 1])
+            conduct_row(head, row, part)
+
+    @pl.loop(0, rows)
+    def _(row):
+        soil_row(row + first, class_in[row])
+        ks[row + first] = 0.5 * ks_in[row]
+        head_a[row + first] = head_in[row]
+
+    pl.semaphore_wait(barrier, count - 1)
+
+    early, late = slice(0, HALO), slice(rows - HALO, rows)
+    above_own = slice(last + 1, total_rows)
+    push(
+        REST,
+        0,
+        head_in.at[early, rest_part],
+        head_in.at[late, rest_part],
+        rest.at[0, 0],
+        rest.at[0, 1],
+    )
+    push(
+        TOPS,
+        0,
+        head_in.at[0 : HALO + 1, top_part],
+        head_in.at[rows - HALO - 1 : rows, top_part],
+        tops.at[0, 0],
+        tops.at[0, 1],
+    )
+    push(SOIL_C, 0, class_in.at[early], class_in.at[late], classes.at[0], classes.at[1])
+    push(SOIL_K, 0, ks_in.at[early], ks_in.at[late], ks.at[0:HALO], ks.at[above_own])
+
+    def spread(away):
+        peer = lax.rem(me + away, count)
+        return pltpu.make_async_remote_copy(
+            src_ref=packed.at[pl.ds(pl.multiple_of(peer * rows, rows), 3 * rows)],
+            dst_ref=gathered.at[me],
+            send_sem=spread_send.at[away],
+            recv_sem=spread_recv.at[away],
+            device_id=at(peer),
+            device_id_type=pl.DeviceIdType.MESH,
+        )
+
+    for away in range(1, count):
+        spread(away).start()
+    gathered[me] = packed[pl.ds(pl.multiple_of(me * rows, rows), 3 * rows)]
 
     own = slice(rows, 2 * rows)
     wide_lane = lax.broadcasted_iota(jnp.int32, (3 * rows, columns), 1)
@@ -298,58 +296,102 @@
             sums.append(total)
         return sums[0], BED_RATE * sums[1]
 
+    def surface_halo(slot):
+        for side in range(HALO):
+            head_a[side, top_part] = tops[slot, 0, side + 1]
+            head_a[last + 1 + side, top_part] = tops[slot, 1, side]
+
+    conduct_rows(head_a, first, last + 1, rest_part)
+
     @pl.loop(0, STEPS)
     def _(step):
         slot = lax.rem(step, 2)
         other = 1 - slot
         going = step < STEPS - 1
 
-        def push_b():
-            push(HEAD_B, head_b.at[1], head_b.at[rows], head_b.at[0], head_b.at[last_row])
-
-        def take_b():
-            await_recv(HEAD_B, head_b.at[0], head_b.at[last_row])
-            await_send(HEAD_B, head_b.at[1], head_b.at[rows])
-
-        def push_a():
-            @pl.when(going)
-            def _():
-                push(HEAD_A, head_a.at[1], head_a.at[rows], head_a.at[0], head_a.at[last_row])
-
-        sweep(head_a, head_b, lambda: None, push_b)
-        sweep(head_b, head_a, take_b, push_a)
+        conduct_rows(head_a, first, last + 1, top_part)
+        for row in range(first + 1, last):
+            flow_row(head_a, head_b, row, row - 1, row + 1)
 
         @pl.when(step == 0)
         def _():
+            settle(TOPS, 0, tops.at[0, 0], tops.at[0, 1])
+            surface_halo(0)
+            settle(SOIL_C, 0, classes.at[0], classes.at[1])
+            settle(SOIL_K, 0, ks.at[0:HALO], ks.at[above_own])
+            for side in range(HALO):
+                for row, found in ((side, classes[0, side]), (last + 1 + side, classes[1, side])):
+                    soil_row(row, found)
+                    ks[row] = 0.5 * ks[row]
+
+        settle(REST, slot, rest.at[slot, 0], rest.at[slot, 1])
+        for side in range(HALO):
+            head_a[side, rest_part] = rest[slot, 0, side]
+            head_a[last + 1 + side, rest_part] = rest[slot, 1, side]
+        conduct_rows(head_a, 0, HALO, whole_part)
+        conduct_rows(head_a, last + 1, total_rows, whole_part)
+        flow_row(head_a, head_b, first, low, first + 1)
+        flow_row(head_a, head_b, last, last - 1, high)
+        flow_row(head_a, head_b, first - 1, first - 2, first)
+        flow_row(head_a, head_b, last + 1, last, last + 2)
+
+        conduct_rows(head_b, first - 1, last + 2, whole_part)
+        for row in range(first, last + 1):
+            if row <= first + HALO or row >= last - HALO:
+                below = low if row == first else row - 1
+                above = high if row == last else row + 1
+                flow_row(head_b, head_a, row, below, above)
+        push(
+            TOPS,
+            other,
+            head_a.at[first : first + HALO + 1, top_part],
+            head_a.at[last - HALO : last + 1, top_part],
+            tops.at[other, 0],
+            tops.at[other, 1],
+        )
+
+        @pl.when(going)
+        def _():
+            push(
+                REST,
+                other,
+                head_a.at[first : first + HALO, rest_part],
+                head_a.at[last - HALO + 1 : last + 1, rest_part],
+                rest.at[other, 0],
+                rest.at[other, 1],
+            )
+
+        for row in range(first + HALO + 1, last - HALO):
+            flow_row(head_b, head_a, row, row - 1, row + 1)
+
+        @pl.when(going)
+        def _():
+            conduct_rows(head_a, first, last + 1, rest_part)
+
+        @pl.when(step == 0)
+        def _():
             assemble()
 
-        low_level = levels.at[slot, 0:rows]
-        own_level = levels.at[slot, own]
-        high_level = levels.at[slot, 2 * rows : 3 * rows]
-
         @pl.when(step > 0)
         def _():
-            await_recv(LEVEL, low_level, high_level)
-            await_send(LEVEL, own_level, own_level)
+            settle(
+                LEVEL, slot, levels.at[slot, 0:rows], levels.at[slot, 2 * rows : 3 * rows]
+            )
 
         for row in range(rows):
-            depths[rows + row : rows + row + 1] = jnp.maximum(head_a[row + 1, 0:1, :], 0.0)
-        low_depth = depths.at[0:rows]
-        own_depth = depths.at[own]
-        high_depth = depths.at[2 * rows : 3 * rows]
-        push(DEPTH, own_depth, own_depth, low_depth, high_depth)
-        await_recv(DEPTH, low_depth, high_depth)
-        await_send(DEPTH, own_depth, own_depth)
-
-        @pl.when(going)
-        def _():
-            await_recv(HEAD_A, head_a.at[0], head_a.at[last_row])
-            await_send(HEAD_A, head_a.at[1], head_a.at[rows])
+            depths[rows + row : rows + row + 1] = jnp.maximum(head_a[row + first, 0:1, :], 0.0)
+        settle(TOPS, other, tops.at[other, 0], tops.at[other, 1])
+        for side in range(HALO + 1):
+            spot = rows - HALO - 1 + side
+            depths[spot : spot + 1] = jnp.maximum(tops[other, 0, side, 0:1, :], 0.0)
+            spot = 2 * rows + side
+            depths[spot : spot + 1] = jnp.maximum(tops[other, 1, side, 0:1, :], 0.0)
 
         change, bed_change = surface(levels[slot], depths[...])
-        for row in range(rows + 2):
-            top = head_a[row, 0:1, :]
-            head_a[row, 0:1, :] = top + change[rows - 1 + row : rows + row]
+        surface_halo(other)
+        for row in range(total_rows):
+            spot = rows - first + row
+            head_a[row, 0:1, :] = head_a[row, 0:1, :] + change[spot : spot + 1]
         levels[other, own] = levels[slot, own] + bed_change[own]
 
         @pl.when(going)
@@ -357,6 +399,7 @@
             next_level = levels.at[other, own]
             push(
                 LEVEL,
+                other,
                 next_level,
                 next_level,
                 levels.at[other, 0:rows],
@@ -380,7 +423,7 @@
     for away in range(1, count):
         finish(away).start()
     final_dst[me] = final_src[me // per]
-    head_out[...] = head_a[1 : rows + 1]
+    head_out[...] = head_a[first : last + 1]
     for away in range(1, count):
         finish(away).wait()
     members = LANES // rows
@@ -415,7 +458,7 @@
     classes = jnp.swapaxes(soil_class, 0, 1).astype(jnp.float32)
     vmem = pl.BlockSpec(memory_space=pltpu.VMEM)
     smem = pl.BlockSpec(memory_space=pltpu.SMEM)
-    wide = pltpu.VMEM((rows + 2, layers, columns), jnp.float32)
+    wide = pltpu.VMEM((rows + 2 * HALO, layers, columns), jnp.float32)
     dma = pltpu.SemaphoreType.DMA
     head_out, bed_out = pl.pallas_call(
         functools.partial(kernel, count),
@@ -437,14 +480,16 @@
             pltpu.VMEM((2, 3 * rows, columns), jnp.float32),
             pltpu.VMEM((3 * rows, columns), jnp.float32),
             pltpu.VMEM((3, 3 * rows, columns), jnp.float32),
-            pltpu.VMEM((2, layers, columns), jnp.float32),
+            pltpu.VMEM((2, HALO, layers, columns), jnp.float32),
+            pltpu.VMEM((2, 2, HALO + 1, TOP, columns), jnp.float32),
+            pltpu.VMEM((2, 2, HALO, layers - TOP, columns), jnp.float32),
             pltpu.VMEM((width + 2 * rows, LANES), jnp.float32),
             pltpu.VMEM((count, 3 * rows, LANES), jnp.float32),
             pltpu.VMEM((columns // LANES, rows, LANES), jnp.float32),
             pltpu.VMEM((count, rows, LANES), jnp.float32),
             pltpu.VMEM((LANES, width), jnp.float32),
-            dma((6, 2)),
-            dma((6, 2)),
+            dma((5, 2, 2)),
+            dma((5, 2, 2)),
             dma((count,)),
             dma((count,)),
             dma((count,)),

time: 57.8 us -> 50.5 us (0.87)
  Pallas kernels: 52.4 us -> 45.1 us
    pallas_call x1, Pallas kernels: 52.4 us -> 45.1 us  [on_device(): pl.pallas_call(functools.partial(kernel, count), out_shape=(jax.ShapeDtyp...]
where the time goes in v1:
time: 50.5 us; the launch traced here: 50.3 us
  Pallas kernels  45.1 us (89%)
  local copies, waits for them, and re-layouts  3 us (6%)
  other arithmetic  1.44 us (3%)
  between operations  0.77 us (2%)
    pallas_call x1, Pallas kernels, on_device(): pl.pallas_call(functools.partial(kernel, count), out_shape=(jax.ShapeDtyp...  45.1 us
    unnamed x24, local copies, waits for them, and re-layouts  2.39 us
    convert_element_type x1, other arithmetic, on_device(): classes = jnp.swapaxes(soil_class, 0, 1).astype(jnp.float32)  1.44 us

profile of v1, /device:TPU:0, one launch (start us, length us, event | category | flops | bytes accessed | tf_op | source)
XLA Modules:
  0.0 50.3 jit_solution(2115023416766109936)
XLA Ops:
  0.6 0.0 copy-start.9
  0.6 0.0 copy-start.10
  0.6 1.4 %fusion.class_in = f32[8,32,512]{2,1,0:T(8,128)S(1)} fusion(s32[32,8,512]{2,1,0:T(8,128)} %param.14), kind=kLoop, calls=%fused_computation.1 | loop fusion | flops 131072 | bytes 1048576 | tf_op jit(solution)/shard_map/convert_element_type | solution.py:458
  2.1 0.0 copy-done.9
  2.1 0.0 copy-done.10
  2.1 0.0 copy-start
  2.1 0.0 copy-start.1
  2.1 0.0 copy-start.2
  2.1 0.0 copy-start.3
  2.2 0.0 copy-start.4
  2.2 0.0 copy-start.8
  2.2 0.6 %copy_bitcast_fusion = (f32[8,32,512]{2,1,0:T(8,128)S(1)}, f32[8,32,512]{2,1,0:T(8,128)S(1)}) fusion(f32[32,8,512]{2,1,0:T(8,128)S(1)} %copy-done.9, f32[32,8,512]{2,1,0:T(8,128)S(1)} %copy-done.10), kind=kLoop, calls=%fused_computation.2 | loop fusion | bytes 2097152 | tf_op jit(solution)/shard_map/transpose | solution.py:457
  2.8 0.0 copy-start.5
  2.8 0.0 copy-start.6
  2.8 0.0 copy-start.7
  2.9 0.0 copy-done.2
  2.9 0.0 copy-done.3
  2.9 0.0 copy-done.4
  2.9 0.6 %copy-done.5 = f32[12]{0:T(128)S(1)} copy-done((f32[12]{0:T(128)S(1)}, f32[12]{0:T(128)}, u32[]{:S(2)}) %copy-start.5) | copy-done | bytes 72
  3.5 0.0 copy-done.6
  3.5 0.0 copy-done.7
  3.5 45.1 %shard_map.131 = (f32[8,32,512]{2,1,0:T(8,128)S(1)}, f32[32,128]{1,0:T(8,128)S(1)}) custom-call(f32[8,32,512]{2,1,0:T(8,128)S(1)} %get-tuple-element.9.head_in, f32[8,32,512]{2,1,0:T(8,128)S(1)} %get-tuple-element.8.ks_in, f32[8,32,512]{2,1,0:T(8,128)S(1)} %fusion.class_in, f32[12]{0:T(128)S(1)} %copy-done.5, f32[12]{0:T(128)S(1)} %copy-done.6, ...), custom_call_target="tpu_custom_call" | custom-call | tf_op jit(solution)/shard_map/pallas_call | solution.py:463
  48.6 1.1 %copy.17 = f32[32,8,512]{2,1,0:T(8,128)} copy(f32[32,8,512]{2,0,1:T(8,128)S(1)} %bitcast.7) | data formatting | bytes 1048576
  49.7 0.6 %copy.24 = f32[32,128]{1,0:T(8,128)} copy(f32[32,128]{1,0:T(8,128)S(1)} %get-tuple-element.13) | data formatting | bytes 32768
  (3 shorter events, 0.0 us)
Async XLA Ops:
  0.6 1.5 %copy-start.9 = (f32[32,8,512]{2,1,0:T(8,128)S(1)}, f32[32,8,512]{2,1,0:T(8,128)}, u32[]{:S(2)}) copy-start(f32[32,8,512]{2,1,0:T(8,128)} %param.13) | copy-start | bytes 1572868
  0.6 1.5 %copy-start.10 = (f32[32,8,512]{2,1,0:T(8,128)S(1)}, f32[32,8,512]{2,1,0:T(8,128)}, u32[]{:S(2)}) copy-start(f32[32,8,512]{2,1,0:T(8,128)} %param.12) | copy-start | bytes 1572868
  2.1 0.7 %copy-start = (f32[32,128]{1,0:T(8,128)S(1)}, f32[32,128]{1,0:T(8,128)}, u32[]{:S(2)}) copy-start(f32[32,128]{1,0:T(8,128)} %bed_in.1) | copy-start | bytes 49156
  2.1 0.7 %copy-start.1 = (s32[32,128]{1,0:T(8,128)S(1)}, s32[32,128]{1,0:T(8,128)}, u32[]{:S(2)}) copy-start(s32[32,128]{1,0:T(8,128)} %code_in.1) | copy-start | bytes 49156
  2.1 0.7 %copy-start.2 = (s32[32,128]{1,0:T(8,128)S(1)}, s32[32,128]{1,0:T(8,128)}, u32[]{:S(2)}) copy-start(s32[32,128]{1,0:T(8,128)} %soil_in.1) | copy-start | bytes 49156
  2.1 0.7 %copy-start.3 = (s32[32,128]{1,0:T(8,128)S(1)}, s32[32,128]{1,0:T(8,128)}, u32[]{:S(2)}) copy-start(s32[32,128]{1,0:T(8,128)} %cover_in.1) | copy-start | bytes 49156
  2.2 0.7 %copy-start.4 = (s32[32,128]{1,0:T(8,128)S(1)}, s32[32,128]{1,0:T(8,128)}, u32[]{:S(2)}) copy-start(s32[32,128]{1,0:T(8,128)} %pond_in.1) | copy-start | bytes 49156
  2.2 0.7 %copy-start.8 = (f32[12]{0:T(128)S(1)}, f32[12]{0:T(128)}, u32[]{:S(2)}) copy-start(f32[12]{0:T(128)} %erod_t.1) | copy-start | bytes 148
  2.8 0.7 %copy-start.5 = (f32[12]{0:T(128)S(1)}, f32[12]{0:T(128)}, u32[]{:S(2)}) copy-start(f32[12]{0:T(128)} %alpha_t.1) | copy-start | bytes 148
  2.8 0.7 %copy-start.6 = (f32[12]{0:T(128)S(1)}, f32[12]{0:T(128)}, u32[]{:S(2)}) copy-start(f32[12]{0:T(128)} %shape_t.1) | copy-start | bytes 148
  2.8 0.7 %copy-start.7 = (f32[17]{0:T(128)S(1)}, f32[17]{0:T(128)}, u32[]{:S(2)}) copy-start(f32[17]{0:T(128)} %convey_t.1) | copy-start | bytes 208

commit v2 on v1

--- a/solution.py
+++ b/solution.py
@@ -17,7 +17,7 @@
 SHIFT_Y = (0, 1, 1, 1, 0, -1, -1, -1)
 TINY = 1.2e-38
 LANES = 128
-TOPS, REST, LEVEL, SOIL_K, SOIL_C = range(5)
+TOPS, REST, LEVEL, SOIL_K, SOIL_C, DEPTH = range(6)
 HALO = 2
 TOP = 8
 
@@ -64,6 +64,9 @@
     classes,
     tops,
     rest,
+    edge,
+    edges,
+    halo_change,
     packed,
     gathered,
     final_src,
@@ -122,20 +125,26 @@
         def _():
             to_right(kind, slot, for_right, low_halo).start()
 
-    def settle(kind, slot, low_halo, high_halo):
+    def settle(kind, slot, low_halo, high_halo, recv=True, send=True):
         @pl.when(has_left)
         def _():
-            to_right(kind, slot, low_halo, low_halo).wait_recv()
-            to_left(kind, slot, low_halo, low_halo).wait_send()
+            if recv:
+                to_right(kind, slot, low_halo, low_halo).wait_recv()
+            if send:
+                to_left(kind, slot, low_halo, low_halo).wait_send()
 
         @pl.when(has_right)
         def _():
-            to_left(kind, slot, high_halo, high_halo).wait_recv()
-            to_right(kind, slot, high_halo, high_halo).wait_send()
+            if recv:
+                to_left(kind, slot, high_halo, high_halo).wait_recv()
+            if send:
+                to_right(kind, slot, high_halo, high_halo).wait_send()
 
     levels[...] = jnp.zeros_like(levels)
     depths[...] = jnp.zeros_like(depths)
-    tops[...] = jnp.zeros_like(tops)
+    edge[...] = jnp.zeros_like(edge)
+    edges[...] = jnp.zeros_like(edges)
+    halo_change[...] = jnp.zeros_like(halo_change)
 
     barrier = pltpu.get_barrier_semaphore()
     for away in range(1, count):
@@ -221,8 +230,8 @@
     push(
         TOPS,
         0,
-        head_in.at[0 : HALO + 1, top_part],
-        head_in.at[rows - HALO - 1 : rows, top_part],
+        head_in.at[early, top_part],
+        head_in.at[late, top_part],
         tops.at[0, 0],
         tops.at[0, 1],
     )
@@ -298,7 +307,7 @@
 
     def surface_halo(slot):
         for side in range(HALO):
-            head_a[side, top_part] = tops[slot, 0, side + 1]
+            head_a[side, top_part] = tops[slot, 0, side]
             head_a[last + 1 + side, top_part] = tops[slot, 1, side]
 
     conduct_rows(head_a, first, last + 1, rest_part)
@@ -315,8 +324,7 @@
 
         @pl.when(step == 0)
         def _():
-            settle(TOPS, 0, tops.at[0, 0], tops.at[0, 1])
-            surface_halo(0)
+            settle(TOPS, 0, tops.at[0, 0], tops.at[0, 1], recv=False)
             settle(SOIL_C, 0, classes.at[0], classes.at[1])
             settle(SOIL_K, 0, ks.at[0:HALO], ks.at[above_own])
             for side in range(HALO):
@@ -324,6 +332,11 @@
                     soil_row(row, found)
                     ks[row] = 0.5 * ks[row]
 
+        settle(TOPS, slot, tops.at[slot, 0], tops.at[slot, 1], send=False)
+        surface_halo(slot)
+        for side in range(HALO):
+            for row, spot in ((side, side), (last + 1 + side, HALO + side)):
+                head_a[row, 0:1, :] = head_a[row, 0:1, :] + halo_change[spot : spot + 1]
         settle(REST, slot, rest.at[slot, 0], rest.at[slot, 1])
         for side in range(HALO):
             head_a[side, rest_part] = rest[slot, 0, side]
@@ -341,17 +354,22 @@
                 below = low if row == first else row - 1
                 above = high if row == last else row + 1
                 flow_row(head_b, head_a, row, below, above)
-        push(
-            TOPS,
-            other,
-            head_a.at[first : first + HALO + 1, top_part],
-            head_a.at[last - HALO : last + 1, top_part],
-            tops.at[other, 0],
-            tops.at[other, 1],
-        )
+        for side in range(HALO + 1):
+            edge[side : side + 1] = jnp.maximum(head_a[first + side, 0:1, :], 0.0)
+            spot = HALO + 1 + side
+            edge[spot : spot + 1] = jnp.maximum(head_a[last - HALO + side, 0:1, :], 0.0)
+        push(DEPTH, other, edge, edge, edges.at[other, 0], edges.at[other, 1])
 
         @pl.when(going)
         def _():
+            push(
+                TOPS,
+                other,
+                head_a.at[first : first + HALO, top_part],
+                head_a.at[last - HALO + 1 : last + 1, top_part],
+                tops.at[other, 0],
+                tops.at[other, 1],
+            )
             push(
                 REST,
                 other,
@@ -380,18 +398,22 @@
 
         for row in range(rows):
             depths[rows + row : rows + row + 1] = jnp.maximum(head_a[row + first, 0:1, :], 0.0)
-        settle(TOPS, other, tops.at[other, 0], tops.at[other, 1])
-        for side in range(HALO + 1):
-            spot = rows - HALO - 1 + side
-            depths[spot : spot + 1] = jnp.maximum(tops[other, 0, side, 0:1, :], 0.0)
-            spot = 2 * rows + side
-            depths[spot : spot + 1] = jnp.maximum(tops[other, 1, side, 0:1, :], 0.0)
+        settle(DEPTH, other, edges.at[other, 0], edges.at[other, 1])
+        span = HALO + 1
+        depths[rows - span : rows] = edges[other, 0, span : 2 * span]
+        depths[2 * rows : 2 * rows + span] = edges[other, 1, 0:span]
 
         change, bed_change = surface(levels[slot], depths[...])
-        surface_halo(other)
-        for row in range(total_rows):
+
+        @pl.when(going)
+        def _():
+            settle(TOPS, other, tops.at[other, 0], tops.at[other, 1], recv=False)
+
+        for row in range(first, last + 1):
             spot = rows - first + row
             head_a[row, 0:1, :] = head_a[row, 0:1, :] + change[spot : spot + 1]
+        halo_change[0:HALO] = change[rows - HALO : rows]
+        halo_change[HALO : 2 * HALO] = change[2 * rows : 2 * rows + HALO]
         levels[other, own] = levels[slot, own] + bed_change[own]
 
         @pl.when(going)
@@ -481,15 +503,18 @@
             pltpu.VMEM((3 * rows, columns), jnp.float32),
             pltpu.VMEM((3, 3 * rows, columns), jnp.float32),
             pltpu.VMEM((2, HALO, layers, columns), jnp.float32),
-            pltpu.VMEM((2, 2, HALO + 1, TOP, columns), jnp.float32),
+            pltpu.VMEM((2, 2, HALO, TOP, columns), jnp.float32),
             pltpu.VMEM((2, 2, HALO, layers - TOP, columns), jnp.float32),
+            pltpu.VMEM((TOP, columns), jnp.float32),
+            pltpu.VMEM((2, 2, TOP, columns), jnp.float32),
+            pltpu.VMEM((TOP, columns), jnp.float32),
             pltpu.VMEM((width + 2 * rows, LANES), jnp.float32),
             pltpu.VMEM((count, 3 * rows, LANES), jnp.float32),
             pltpu.VMEM((columns // LANES, rows, LANES), jnp.float32),
             pltpu.VMEM((count, rows, LANES), jnp.float32),
             pltpu.VMEM((LANES, width), jnp.float32),
-            dma((5, 2, 2)),
-            dma((5, 2, 2)),
+            dma((6, 2, 2)),
+            dma((6, 2, 2)),
             dma((count,)),
             dma((count,)),
             dma((count,)),

time: 50.5 us -> 50.1 us (level)
  no operation moved by 1% of the time
where the time goes in v2:
time: 50.1 us; the launch traced here: 49.8 us
  Pallas kernels  44.6 us (89%)
  local copies, waits for them, and re-layouts  3 us (6%)
  other arithmetic  1.44 us (3%)
  between operations  0.77 us (2%)
    pallas_call x1, Pallas kernels, on_device(): pl.pallas_call(functools.partial(kernel, count), out_shape=(jax.ShapeDtyp...  44.6 us
    unnamed x24, local copies, waits for them, and re-layouts  2.39 us
    convert_element_type x1, other arithmetic, on_device(): classes = jnp.swapaxes(soil_class, 0, 1).astype(jnp.float32)  1.44 us

profile of v2, /device:TPU:0, one launch (start us, length us, event | category | flops | bytes accessed | tf_op | source)
XLA Modules:
  0.0 49.8 jit_solution(4980917118213146583)
XLA Ops:
  0.6 0.0 copy-start.9
  0.6 0.0 copy-start.10
  0.6 1.4 %fusion.class_in = f32[8,32,512]{2,1,0:T(8,128)S(1)} fusion(s32[32,8,512]{2,1,0:T(8,128)} %param.14), kind=kLoop, calls=%fused_computation.1 | loop fusion | flops 131072 | bytes 1048576 | tf_op jit(solution)/shard_map/convert_element_type | solution.py:480
  2.1 0.0 copy-done.9
  2.1 0.0 copy-done.10
  2.1 0.0 copy-start
  2.1 0.0 copy-start.1
  2.1 0.0 copy-start.2
  2.1 0.0 copy-start.3
  2.2 0.0 copy-start.4
  2.2 0.0 copy-start.8
  2.2 0.6 %copy_bitcast_fusion = (f32[8,32,512]{2,1,0:T(8,128)S(1)}, f32[8,32,512]{2,1,0:T(8,128)S(1)}) fusion(f32[32,8,512]{2,1,0:T(8,128)S(1)} %copy-done.9, f32[32,8,512]{2,1,0:T(8,128)S(1)} %copy-done.10), kind=kLoop, calls=%fused_computation.2 | loop fusion | bytes 2097152 | tf_op jit(solution)/shard_map/transpose | solution.py:479
  2.8 0.0 copy-start.5
  2.8 0.0 copy-start.6
  2.8 0.0 copy-start.7
  2.9 0.0 copy-done.2
  2.9 0.0 copy-done.3
  2.9 0.0 copy-done.4
  2.9 0.6 %copy-done.5 = f32[12]{0:T(128)S(1)} copy-done((f32[12]{0:T(128)S(1)}, f32[12]{0:T(128)}, u32[]{:S(2)}) %copy-start.5) | copy-done | bytes 72
  3.5 0.0 copy-done.6
  3.5 0.0 copy-done.7
  3.5 44.6 %shard_map.131 = (f32[8,32,512]{2,1,0:T(8,128)S(1)}, f32[32,128]{1,0:T(8,128)S(1)}) custom-call(f32[8,32,512]{2,1,0:T(8,128)S(1)} %get-tuple-element.9.head_in, f32[8,32,512]{2,1,0:T(8,128)S(1)} %get-tuple-element.8.ks_in, f32[8,32,512]{2,1,0:T(8,128)S(1)} %fusion.class_in, f32[12]{0:T(128)S(1)} %copy-done.5, f32[12]{0:T(128)S(1)} %copy-done.6, ...), custom_call_target="tpu_custom_call" | custom-call | tf_op jit(solution)/shard_map/pallas_call | solution.py:485
  48.1 1.1 %copy.17 = f32[32,8,512]{2,1,0:T(8,128)} copy(f32[32,8,512]{2,0,1:T(8,128)S(1)} %bitcast.7) | data formatting | bytes 1048576
  49.2 0.6 %copy.24 = f32[32,128]{1,0:T(8,128)} copy(f32[32,128]{1,0:T(8,128)S(1)} %get-tuple-element.13) | data formatting | bytes 32768
  (3 shorter events, 0.0 us)
Async XLA Ops:
  0.6 1.5 %copy-start.9 = (f32[32,8,512]{2,1,0:T(8,128)S(1)}, f32[32,8,512]{2,1,0:T(8,128)}, u32[]{:S(2)}) copy-start(f32[32,8,512]{2,1,0:T(8,128)} %param.13) | copy-start | bytes 1572868
  0.6 1.5 %copy-start.10 = (f32[32,8,512]{2,1,0:T(8,128)S(1)}, f32[32,8,512]{2,1,0:T(8,128)}, u32[]{:S(2)}) copy-start(f32[32,8,512]{2,1,0:T(8,128)} %param.12) | copy-start | bytes 1572868
  2.1 0.7 %copy-start = (f32[32,128]{1,0:T(8,128)S(1)}, f32[32,128]{1,0:T(8,128)}, u32[]{:S(2)}) copy-start(f32[32,128]{1,0:T(8,128)} %bed_in.1) | copy-start | bytes 49156
  2.1 0.7 %copy-start.1 = (s32[32,128]{1,0:T(8,128)S(1)}, s32[32,128]{1,0:T(8,128)}, u32[]{:S(2)}) copy-start(s32[32,128]{1,0:T(8,128)} %code_in.1) | copy-start | bytes 49156
  2.1 0.7 %copy-start.2 = (s32[32,128]{1,0:T(8,128)S(1)}, s32[32,128]{1,0:T(8,128)}, u32[]{:S(2)}) copy-start(s32[32,128]{1,0:T(8,128)} %soil_in.1) | copy-start | bytes 49156
  2.1 0.7 %copy-start.3 = (s32[32,128]{1,0:T(8,128)S(1)}, s32[32,128]{1,0:T(8,128)}, u32[]{:S(2)}) copy-start(s32[32,128]{1,0:T(8,128)} %cover_in.1) | copy-start | bytes 49156
  2.2 0.7 %copy-start.4 = (s32[32,128]{1,0:T(8,128)S(1)}, s32[32,128]{1,0:T(8,128)}, u32[]{:S(2)}) copy-start(s32[32,128]{1,0:T(8,128)} %pond_in.1) | copy-start | bytes 49156
  2.2 0.7 %copy-start.8 = (f32[12]{0:T(128)S(1)}, f32[12]{0:T(128)}, u32[]{:S(2)}) copy-start(f32[12]{0:T(128)} %erod_t.1) | copy-start | bytes 148
  2.8 0.7 %copy-start.5 = (f32[12]{0:T(128)S(1)}, f32[12]{0:T(128)}, u32[]{:S(2)}) copy-start(f32[12]{0:T(128)} %alpha_t.1) | copy-start | bytes 148
  2.8 0.7 %copy-start.6 = (f32[12]{0:T(128)S(1)}, f32[12]{0:T(128)}, u32[]{:S(2)}) copy-start(f32[12]{0:T(128)} %shape_t.1) | copy-start | bytes 148
  2.8 0.7 %copy-start.7 = (f32[17]{0:T(128)S(1)}, f32[17]{0:T(128)}, u32[]{:S(2)}) copy-start(f32[17]{0:T(128)} %convey_t.1) | copy-start | bytes 208
